TPU v7x, 768 devices: a whole 4x8x12 slice. The times are simulated.
768 devices in a mesh: dp: 48 (over y_lo, z), mp: 16 (over y_hi, x, core).
Axes of the slice: x: 4, y: 8 (y_hi: 2, y_lo: 4; y = y_hi * 4 + y_lo), z: 12, core: 2. Of those that a mesh axis runs over, the one named last changes fastest.
Arguments:
- output_gradient: bfloat16 [9216, 3584], P('dp', 'mp'), may hold values from -6 to 6
- gate_preactivation: bfloat16 [9216, 9984], P('dp', 'mp'), may hold values from -8 to 8
- up_preactivation: bfloat16 [9216, 9984], P('dp', 'mp'), may hold values from -6 to 6
- down_weight: bfloat16 [9984, 3584], P('mp'), may hold values from -0.0625 to 0.0625
- adapter_first: bfloat16 [9984, 96], P('mp'), may hold values from -0.0625 to 0.0625
- adapter_second: bfloat16 [96, 3584], replicated, may hold values from -0.09375 to 0.09375
- plan: int32 [1152], P('dp'), may hold values from 0 to 47, as said below
Outputs:
- grad_gate: bfloat16 [9216, 9984], P('dp', 'mp')
- grad_up: bfloat16 [9216, 9984], P('dp', 'mp')
- grad_a: float32 [16, 624, 96], P('mp', 'dp')
- grad_b: float32 [96, 3584], P('dp')
Inputs may be any that keep to these rules, and one draw needn't show every extreme that they name: Every owner 0 to 47 is named by exactly 24 blocks; of the 24 blocks of one device (plan rows of one index of dp) at most 1 name the same owner, and in every draw some device's blocks name one owner exactly 1 times.
All inputs are finite; a program needn't handle non-finite values.
Results may differ from a plain program's by a relative error of at most 0.005.
Values may be sent and summed in bfloat16 or wider, within the bound.
A program may use at most 32 MiB of HBM per device.

v0:
```python
import math

import jax
import jax.numpy as jnp
from jax import lax
from jax.sharding import PartitionSpec as P


def in_one_piece(arrays, axis, split_dim, concat_dim, along):
    widths = [math.prod(a.shape[along:]) for a in arrays]
    both = jnp.concatenate(
        [a.reshape(*a.shape[:along], w) for a, w in zip(arrays, widths)], axis=along
    )
    result = lax.all_to_all(both, axis, split_axis=split_dim, concat_axis=concat_dim, tiled=True)
    pieces = jnp.split(result, [sum(widths[:k]) for k in range(1, len(widths))], axis=along)
    return tuple(
        (b.reshape(*result.shape[:along], *a.shape[along:]) for a, b in zip(arrays, pieces))
    )


def joined_along(pieces, dim):
    lengths = list(pieces.shape[1:])
    lengths[dim] *= pieces.shape[0]
    return jnp.moveaxis(pieces, 0, dim).reshape(lengths)


def copy_for_each(array, axis):
    count = lax.axis_size(axis)
    return lax.all_to_all(
        jnp.broadcast_to(array[None], (count, *array.shape)), axis, 0, 0, tiled=True
    )


def gather_directly(array, axis, dim):
    return joined_along(copy_for_each(array, axis), dim)


def over_copies(array, axis):
    return copy_for_each(array, axis).sum(axis=0)


def split_up(array, dim, count):
    lengths = array.shape
    pieces = array.reshape(*lengths[:dim], count, lengths[dim] // count, *lengths[dim + 1 :])
    return jnp.moveaxis(pieces, dim, 0)


def sum_at_owner(array, axis, dim):
    pieces = split_up(array, dim, lax.axis_size(axis))
    arrived = lax.all_to_all(pieces, axis, split_axis=0, concat_axis=0, tiled=True)
    return arrived.sum(axis=0)


def body(
    output_gradient,
    gate_preactivation,
    up_preactivation,
    down_weight,
    adapter_first,
    adapter_second,
    plan,
):
    groups = lax.axis_size("dp")
    owned = plan.shape[0]
    capacity = -(-owned // groups)
    tokens_here = output_gradient.shape[0]
    feature_cols = output_gradient.shape[1]
    block_width = tokens_here // owned * feature_cols
    slot_count = groups * capacity
    positions = jnp.arange(owned, dtype=jnp.int32)
    earlier = (plan[None, :] == plan[:, None]) & (positions[None, :] < positions[:, None])
    target = plan * capacity + jnp.sum(earlier.astype(jnp.int32), axis=1)
    sending = target[None, :] == jnp.arange(slot_count, dtype=jnp.int32)[:, None]
    outgoing = jnp.dot(
        sending.astype(jnp.bfloat16),
        output_gradient.reshape(owned, block_width),
        preferred_element_type=jnp.float32,
    ).astype(jnp.bfloat16)
    filled = jnp.sum(sending.astype(jnp.float32), axis=1).astype(jnp.bfloat16)
    arrived, present = in_one_piece((outgoing, filled), "dp", 0, 0, 1)
    present_flag = present.astype(jnp.int32)
    ranking = jnp.cumsum(present_flag) - 1
    keeping = (ranking[None, :] == positions[:, None]) & (present_flag[None, :] > 0)
    packed_tokens = (
        jnp.dot(keeping.astype(jnp.bfloat16), arrived, preferred_element_type=jnp.float32)
        .astype(jnp.bfloat16)
        .reshape(tokens_here, feature_cols)
    )
    feature_rows = gather_directly(packed_tokens, "mp", 1)
    gate_vals = gate_preactivation.astype(jnp.float32)
    up_vals = up_preactivation.astype(jnp.float32)
    sigmoid_gate = jax.nn.sigmoid(gate_vals)
    silu_gate = gate_vals * sigmoid_gate
    hidden_units = (silu_gate * up_vals).astype(jnp.bfloat16)
    low_rank_piece = jnp.dot(hidden_units, adapter_first, preferred_element_type=jnp.float32)
    low_rank_rows = over_copies(low_rank_piece, "mp").astype(jnp.bfloat16)
    passed_through = lax.dot_general(
        feature_rows, adapter_second, (((1,), (1,)), ((), ())), preferred_element_type=jnp.float32
    ).astype(jnp.bfloat16)
    grad_a_rows = sum_at_owner(
        lax.dot_general(
            hidden_units,
            passed_through,
            (((0,), (0,)), ((), ())),
            preferred_element_type=jnp.float32,
        ),
        "dp",
        0,
    )
    part_rows = sum_at_owner(
        lax.dot_general(
            low_rank_rows,
            packed_tokens,
            (((0,), (0,)), ((), ())),
            preferred_element_type=jnp.float32,
        ),
        "dp",
        0,
    )
    grad_b_rows = gather_directly(part_rows, "mp", 1)
    hidden_gradient = lax.dot_general(
        feature_rows, down_weight, (((1,), (1,)), ((), ())), preferred_element_type=jnp.float32
    )
    hidden_gradient = hidden_gradient + lax.dot_general(
        passed_through, adapter_first, (((1,), (1,)), ((), ())), preferred_element_type=jnp.float32
    )
    grad_gate = (
        hidden_gradient * up_vals * sigmoid_gate * (1.0 + gate_vals * (1.0 - sigmoid_gate))
    ).astype(jnp.bfloat16)
    grad_up = (hidden_gradient * silu_gate).astype(jnp.bfloat16)
    return (grad_gate, grad_up, grad_a_rows[None], grad_b_rows)


def solution(mesh):
    return jax.shard_map(
        body,
        mesh=mesh,
        in_specs=(
            P("dp", "mp"),
            P("dp", "mp"),
            P("dp", "mp"),
            P("mp", None),
            P("mp", None),
            P(),
            P("dp"),
        ),
        out_specs=(P("dp", "mp"), P("dp", "mp"), P("mp", "dp", None), P("dp", None)),
        check_vma=False,
    )
```

profile of v0, /device:TPU:1, one launch (start us, length us, event | category | flops | bytes accessed | tf_op | source)
XLA Modules:
  0.0 215.2 jit_solution(12652859556015652065)
XLA Ops:
  0.6 0.0 copy-start
  0.6 0.9 convert_reduce_fusion.1
  1.6 0.7 add.18
  2.2 1.0 reshape.73
  3.3 0.1 convert_reduce_fusion
  3.4 0.3 convolution_convert_fusion
  3.7 0.1 copy.28
  3.8 0.3 copy.29
  4.1 37.6 %all_to_all.37 = bf16[48,1,1793]{2,1,0:T(2,128)(2,1)S(1)} all-to-all(bf16[48,1,1793]{2,1,0:T(2,128)(2,1)S(1)} %copy.29), channel_id=1, replica_groups=mesh['dp'=48,'mp'=16] {'dp'}, dimensions={0} | all-to-all | bytes 344256 | tf_op jit(solution)/shard_map/all_to_all | solution.py:14
  41.7 0.1 compare_reduce_fusion
  41.8 0.1 reduce-window.8
  41.9 0.1 add_reduce_fusion
  42.0 0.2 convolution_convert_fusion.1
  42.2 0.2 broadcast_in_dim.10
  42.4 0.1 broadcast_in_dim.11
  42.5 40.0 %all_to_all.38 = bf16[16,192,224]{2,1,0:T(8,128)(2,1)S(1)} all-to-all(bf16[16,192,224]{2,1,0:T(8,128)(2,1)S(1)} %broadcast_in_dim.11), channel_id=1, replica_groups=mesh['dp'=48,'mp'=16] {'mp'}, dimensions={0} | all-to-all | bytes 2752512 | tf_op jit(solution)/shard_map/all_to_all | solution.py:29
  82.5 2.0 copy.30
  84.6 3.5 %reshape.74 = bf16[192,3584]{1,0:T(8,128)(2,1)S(1)} reshape(bf16[192,16,224]{2,1,0:T(8,128)(2,1)} %copy.30) | data formatting | bytes 2752512 | tf_op jit(solution)/shard_map/reshape | solution.py:24
  88.1 0.0 copy-done
  88.1 0.5 convolution_convert_fusion.2
  88.6 0.0 copy-start.1
  88.6 0.0 copy-start.2
  88.6 0.0 copy-start.3
  88.6 4.0 %fusion.17 = f32[192,624]{1,0:T(8,128)S(1)} fusion(bf16[192,3584]{1,0:T(8,128)(2,1)S(1)} %reshape.74, bf16[624,3584]{1,0:T(8,128)(2,1)} %param.10), kind=kOutput, calls=%fused_computation.38 | convolution fusion | flops 858783744 | bytes 6328320 | tf_op jit(solution)/shard_map/dot_general | solution.py:121
  92.6 0.0 copy-done.1
  92.6 0.0 copy-done.2
  92.6 0.0 copy-done.3
  92.6 1.2 multiply_convert_fusion
  93.8 0.2 fusion.19
  94.0 1.3 broadcast_in_dim.13
  95.3 13.6 %all-to-all-start.3 = ((f32[16,192,96]{2,1,0:T(8,128)}), f32[16,192,96]{2,1,0:T(8,128)S(1)}, u32[]{:S(2)}, u32[]{:S(2)}) async-start(f32[16,192,96]{2,1,0:T(8,128)} %broadcast_in_dim.13), calls=%async_computation.3 | async-start | bytes 3145728 | tf_op jit(solution)/shard_map/all_to_all | solution.py:29
  108.9 0.2 reshape.77
  109.1 25.1 %all-to-all-done.3 = f32[16,192,96]{2,1,0:T(8,128)S(1)} async-done(((f32[16,192,96]{2,1,0:T(8,128)}), f32[16,192,96]{2,1,0:T(8,128)S(1)}, u32[]{:S(2)}, u32[]{:S(2)}) %all-to-all-start.3) | async-done | bytes 1179680 | tf_op jit(solution)/shard_map/all_to_all | solution.py:29
  134.2 0.1 reduce_sum.48
  134.3 0.1 copy.32
  134.5 0.1 fusion.9
  134.6 0.7 copy.34
  135.3 24.6 %all-to-all-start.4 = ((f32[48,2,224]{2,1,0:T(2,128)}), f32[48,2,224]{2,1,0:T(2,128)S(1)}, u32[]{:S(2)}, u32[]{:S(2)}) async-start(f32[48,2,224]{2,1,0:T(2,128)} %copy.34), calls=%async_computation.4 | async-start | bytes 196608 | tf_op jit(solution)/shard_map/all_to_all | solution.py:50
  159.9 0.3 fusion.18
  160.2 0.8 reshape.75
  161.0 11.1 %all-to-all-done.4 = f32[48,2,224]{2,1,0:T(2,128)S(1)} async-done(((f32[48,2,224]{2,1,0:T(2,128)}), f32[48,2,224]{2,1,0:T(2,128)S(1)}, u32[]{:S(2)}, u32[]{:S(2)}) %all-to-all-start.4) | async-done | bytes 86048 | tf_op jit(solution)/shard_map/all_to_all | solution.py:50
  172.1 4.5 %all-to-all-start.2 = ((f32[48,13,96]{2,1,0:T(8,128)}), f32[48,13,96]{2,1,0:T(8,128)S(1)}, u32[]{:S(2)}, u32[]{:S(2)}) async-start(f32[48,13,96]{2,1,0:T(8,128)} %reshape.75), calls=%async_computation.2 | async-start | bytes 786432 | tf_op jit(solution)/shard_map/all_to_all | solution.py:50
  176.7 0.1 reduce_sum.49
  176.8 16.3 %all-to-all-done.2 = f32[48,13,96]{2,1,0:T(8,128)S(1)} async-done(((f32[48,13,96]{2,1,0:T(8,128)}), f32[48,13,96]{2,1,0:T(8,128)S(1)}, u32[]{:S(2)}, u32[]{:S(2)}) %all-to-all-start.2) | async-done | bytes 239648 | tf_op jit(solution)/shard_map/all_to_all | solution.py:50
  193.1 0.6 broadcast_in_dim.14
  193.7 11.1 %all-to-all-start.5 = ((f32[16,2,224]{2,1,0:T(2,128)}), f32[16,2,224]{2,1,0:T(2,128)S(1)}, u32[]{:S(2)}, u32[]{:S(2)}) async-start(f32[16,2,224]{2,1,0:T(2,128)} %broadcast_in_dim.14), calls=%async_computation.5 | async-start | bytes 65536 | tf_op jit(solution)/shard_map/all_to_all | solution.py:29
  204.8 0.1 reduce_sum.47
  204.8 0.6 broadcast_in_dim.12
  205.4 9.0 %all-to-all-done.5 = f32[16,2,224]{2,1,0:T(2,128)S(1)} async-done(((f32[16,2,224]{2,1,0:T(2,128)}), f32[16,2,224]{2,1,0:T(2,128)S(1)}, u32[]{:S(2)}, u32[]{:S(2)}) %all-to-all-start.5) | async-done | bytes 28704 | tf_op jit(solution)/shard_map/all_to_all | solution.py:29
  214.5 0.7 reshape.76
  (5 shorter events, 0.1 us)
Async XLA Ops:
  0.6 87.4 %copy-start = (bf16[96,3584]{1,0:T(8,128)(2,1)S(1)}, bf16[96,3584]{1,0:T(8,128)(2,1)}, u32[]{:S(2)}) copy-start(bf16[96,3584]{1,0:T(8,128)(2,1)} %param.12) | copy-start | bytes 2064388
  88.6 4.0 %copy-start.1 = (bf16[624,96]{0,1:T(8,128)(2,1)S(1)}, bf16[624,96]{0,1:T(8,128)(2,1)}, u32[]{:S(2)}) copy-start(bf16[624,96]{0,1:T(8,128)(2,1)} %param.11) | copy-start | bytes 359428
  88.6 4.0 %copy-start.2 = (bf16[192,624]{1,0:T(8,128)(2,1)S(1)}, bf16[192,624]{1,0:T(8,128)(2,1)}, u32[]{:S(2)}) copy-start(bf16[192,624]{1,0:T(8,128)(2,1)} %param.8) | copy-start | bytes 718852
  88.6 4.0 %copy-start.3 = (bf16[192,624]{1,0:T(8,128)(2,1)S(1)}, bf16[192,624]{1,0:T(8,128)(2,1)}, u32[]{:S(2)}) copy-start(bf16[192,624]{1,0:T(8,128)(2,1)} %param.9) | copy-start | bytes 718852
  95.3 38.9 %all-to-all-start.3 = ((f32[16,192,96]{2,1,0:T(8,128)}), f32[16,192,96]{2,1,0:T(8,128)S(1)}, u32[]{:S(2)}, u32[]{:S(2)}) async-start(f32[16,192,96]{2,1,0:T(8,128)} %broadcast_in_dim.13), calls=%async_computation.3 | async-start | bytes 3145728 | tf_op jit(solution)/shard_map/all_to_all | solution.py:29
  135.3 36.8 %all-to-all-start.4 = ((f32[48,2,224]{2,1,0:T(2,128)}), f32[48,2,224]{2,1,0:T(2,128)S(1)}, u32[]{:S(2)}, u32[]{:S(2)}) async-start(f32[48,2,224]{2,1,0:T(2,128)} %copy.34), calls=%async_computation.4 | async-start | bytes 196608 | tf_op jit(solution)/shard_map/all_to_all | solution.py:50
  172.1 20.9 %all-to-all-start.2 = ((f32[48,13,96]{2,1,0:T(8,128)}), f32[48,13,96]{2,1,0:T(8,128)S(1)}, u32[]{:S(2)}, u32[]{:S(2)}) async-start(f32[48,13,96]{2,1,0:T(8,128)} %reshape.75), calls=%async_computation.2 | async-start | bytes 786432 | tf_op jit(solution)/shard_map/all_to_all | solution.py:50
  193.7 20.8 %all-to-all-start.5 = ((f32[16,2,224]{2,1,0:T(2,128)}), f32[16,2,224]{2,1,0:T(2,128)S(1)}, u32[]{:S(2)}, u32[]{:S(2)}) async-start(f32[16,2,224]{2,1,0:T(2,128)} %broadcast_in_dim.14), calls=%async_computation.5 | async-start | bytes 65536 | tf_op jit(solution)/shard_map/all_to_all | solution.py:29
where the time goes:
time: 216 us; the launch traced here: 215 us
  blocking collectives  77.6 us (36%)
  waiting for transfers between devices  61.6 us (29%)
  starting transfers between devices  53.8 us (25%)
  local copies, waits for them, and re-layouts  12.3 us (6%)
  matrix products  6.75 us (3%)
  other arithmetic  2.24 us (1%)
    all_to_all x1, blocking collectives, copy_for_each(): lax.all_to_all(jnp.broadcast_to(array[None], (count, *array.shape)), axis...  40 us
    all_to_all x1, blocking collectives, in_one_piece(): lax.all_to_all(both, axis, split_axis=split_dim, concat_axis=concat_dim,...  37.6 us
    all_to_all x2, waiting for transfers between devices, copy_for_each(): lax.all_to_all(jnp.broadcast_to(array[None], (count, *array.shape)), axis...  34.2 us
    all_to_all x2, starting transfers between devices, sum_at_owner(): lax.all_to_all(pieces, axis, split_axis=0, concat_axis=0, tiled=True)  29.1 us
    all_to_all x2, waiting for transfers between devices, sum_at_owner(): lax.all_to_all(pieces, axis, split_axis=0, concat_axis=0, tiled=True)  27.5 us
    all_to_all x2, starting transfers between devices, copy_for_each(): lax.all_to_all(jnp.broadcast_to(array[None], (count, *array.shape)), axis...  24.7 us
  transfers between devices with their start and end apart: 4, of which 4 were waited for; matrix products, arithmetic and copies ran while one was open for 1% of the time, Pallas kernels for 0%

commit v1 on v0

v1 whole, which is shorter than its diff:
```python
import jax
import jax.numpy as jnp
from jax import lax
from jax.experimental import pallas as pl
from jax.experimental.pallas import tpu as pltpu
from jax.sharding import PartitionSpec as P

MESH = pl.DeviceIdType.MESH
F32, BF16 = jnp.float32, jnp.bfloat16
DP, MP = 48, 16
TOK, FEAT, WIDE = 192, 224, 256
HID, RANK, RW = 624, 96, 128
PIECE = 13
MODEL = 3584


def dot_nn(a, b):
    return lax.dot_general(a, b, (((1,), (0,)), ((), ())), preferred_element_type=F32)


def dot_nt(a, b):
    return lax.dot_general(a, b, (((1,), (1,)), ((), ())), preferred_element_type=F32)


def dot_tn(a, b):
    return lax.dot_general(a, b, (((0,), (0,)), ((), ())), preferred_element_type=F32)


def iota(shape, dim):
    return lax.broadcasted_iota(jnp.int32, shape, dim)


def onehot(cond):
    return jnp.where(cond, 1.0, 0.0).astype(BF16)


def wait_bytes(ref, sem):
    pltpu.make_async_copy(ref, ref, sem).wait()


def kernel(
    og_hbm, gate_hbm, up_hbm, w_hbm, a1_hbm, a2_hbm, plan_hbm,
    gg_hbm, gu_hbm, ga_ref, gb_ref,
    og, og_ext, gate, up, w, a1, a2, plan,
    slots_out, slots_in, low_out, low_in, low_all,
    chunks, weights, acc, c_gate, c_up, hidden_t, earlier, gg, gu,
    b_part, b_out, b_in, b_all, a_out, a_in,
    load_sem, store_sem, g_recv, sems,
):
    me, mm = lax.axis_index("dp"), lax.axis_index("mp")
    (p_send, p_recv, l_send, l_recv, lg_send, lg_recv, g_send, b_send, b_recv,
     bg_send, bg_recv, r_send, r_recv) = [sems.at[k] for k in range(13)]

    barrier = pltpu.get_barrier_semaphore()

    @pl.loop(1, DP)
    def _(i):
        pl.semaphore_signal(
            barrier, inc=1, device_id={"dp": lax.rem(me + i, DP)}, device_id_type=MESH
        )

    @pl.loop(1, MP)
    def _(i):
        pl.semaphore_signal(
            barrier, inc=1, device_id={"mp": lax.rem(mm + i, MP)}, device_id_type=MESH
        )

    loads = [
        pltpu.make_async_copy(src, dst, load_sem.at[k])
        for k, (src, dst) in enumerate(
            [(plan_hbm, plan), (og_hbm, og), (gate_hbm, gate), (up_hbm, up),
             (a1_hbm, a1), (a2_hbm, a2), (w_hbm, w)]
        )
    ]
    for copy in loads:
        copy.start()

    def exchange(axis, count, mine, src, dst, send_sem, recv_sem, by_peer):
        @pl.loop(1, count)
        def _(i):
            peer = lax.rem(mine + i, count)
            pltpu.make_async_remote_copy(
                src_ref=src.at[peer] if by_peer else src.at[mine],
                dst_ref=dst.at[mine],
                send_sem=send_sem,
                recv_sem=recv_sem,
                device_id={axis: peer},
                device_id_type=MESH,
            ).start()

    loads[0].wait()
    expand = onehot(iota((24, TOK), 0) == (iota((24, TOK), 1) >> 3))
    plan_rows = jnp.broadcast_to(plan[...].astype(F32), (8, 24)).astype(BF16)
    owner_of = dot_nn(plan_rows, expand)[0:1, :]
    place = (iota((DP * 8, TOK), 0) >> 3).astype(F32)
    same_row = (iota((DP * 8, TOK), 0) & 7) == (iota((DP * 8, TOK), 1) & 7)
    sending = onehot((owner_of == place) & same_row)
    loads[1].wait()
    og_ext[:, :FEAT] = og[...]
    og_ext[:, FEAT:] = jnp.ones((TOK, WIDE - FEAT), BF16)
    slots_out[...] = dot_nn(sending, og_ext[...]).astype(BF16).reshape(DP, 8, WIDE)
    slots_in[me] = slots_out[me]

    pl.semaphore_wait(barrier, DP - 1 + MP - 1)
    exchange("dp", DP, me, slots_out, slots_in, p_send, p_recv, True)

    loads[2].wait()
    loads[3].wait()
    g = gate[...].astype(F32)
    u = up[...].astype(F32)
    sig = jax.nn.sigmoid(g)
    silu = g * sig
    c_up[...] = silu
    c_gate[...] = u * sig * (1.0 + g * (1.0 - sig))
    hidden = (silu * u).astype(BF16)
    loads[4].wait()
    low_out[...] = jnp.zeros((MP, 16, RW), F32)
    low_out[0 : TOK // 16, :, :RANK] = dot_nn(hidden, a1[...]).reshape(TOK // 16, 16, RANK)
    low_in[mm] = low_out[mm]
    exchange("mp", MP, mm, low_out, low_in, l_send, l_recv, True)

    row = iota((DP * 16, HID), 0)
    spread = onehot(((row >> 4) * PIECE + (row & 15) == iota((DP * 16, HID), 1)) & ((row & 15) < PIECE))
    hidden_t[...] = dot_nt(spread, hidden).astype(BF16)
    first = iota((DP * 8, DP * 8), 0)
    earlier[...] = onehot(((first >> 3) < (iota((DP * 8, DP * 8), 1) >> 3)) & ((first & 7) == 0))

    loads[5].wait()
    loads[6].wait()
    for k in range(MP):
        cols = slice(k * FEAT, (k + 1) * FEAT)
        weights[k, RANK:RW, :] = jnp.zeros((RW - RANK, WIDE), BF16)
        weights[k, :, FEAT:] = jnp.zeros((RW + HID, WIDE - FEAT), BF16)
        weights[k, 0:RANK, :FEAT] = a2[:, cols]
        weights[k, RW:, :FEAT] = w[:, cols]

    wait_bytes(low_in.at[pl.ds(0, MP - 1)], l_recv)
    low_all[mm] = jnp.sum(low_in[...], axis=0).astype(BF16)
    exchange("mp", MP, mm, low_all, low_all, lg_send, lg_recv, False)

    wait_bytes(slots_in.at[pl.ds(0, DP - 1)], p_recv)
    arrived = slots_in[...].reshape(DP * 8, WIDE)
    pick = onehot(iota((8, WIDE), 1) == FEAT)
    present = dot_nt(pick, arrived)
    rank = dot_nn(present.astype(BF16), earlier[...])
    place = (iota((TOK, DP * 8), 0) >> 3).astype(F32)
    same_row = (iota((TOK, DP * 8), 0) & 7) == (iota((TOK, DP * 8), 1) & 7)
    keeping = onehot((present[0:1, :] > 0.5) & (rank[0:1, :] == place) & same_row)
    packed = dot_nn(keeping, arrived).astype(BF16)
    chunks[mm] = packed

    h, x, c = mm // 8, lax.rem(mm // 2, 4), lax.rem(mm, 2)
    o, s = 1 - h, 1 - c
    ahead = lax.rem(x + 5 - 2 * c, 4)
    behind = lax.rem(x + 3 + 2 * c, 4)
    across = lax.rem(x + 2, 4)

    def at(hh, xx, cc):
        return hh * 8 + xx * 2 + cc

    def send(slot, dest):
        pltpu.make_async_remote_copy(
            src_ref=chunks.at[slot],
            dst_ref=chunks.at[slot],
            send_sem=g_send,
            recv_sem=g_recv.at[slot],
            device_id={"mp": dest},
            device_id_type=MESH,
        ).start()

    def arrive(slot):
        wait_bytes(chunks.at[slot], g_recv.at[slot])

    def consume(slot):
        acc[...] += dot_nt(chunks[slot], weights[slot])

    sibling = at(h, x, s)
    send(mm, at(o, x, c))
    send(mm, at(h, ahead, c))
    send(mm, at(h, behind, c))
    send(mm, sibling)
    acc[...] = dot_nt(chunks[mm], weights[mm])

    wait_bytes(low_all.at[pl.ds(0, MP - 1)], lg_recv)
    low = low_all[...].reshape(MP * 16, RW)[:TOK, :]
    b_part[...] = dot_tn(low, packed)
    for k in range(DP):
        b_out[k] = b_part[2 * k : 2 * k + 2, :]
    b_in[me] = b_out[me]
    exchange("dp", DP, me, b_out, b_in, b_send, b_recv, True)

    for hh in (h, o):
        if hh is o:
            arrive(at(o, x, c))
            send(at(o, x, c), at(h, ahead, c))
            send(at(o, x, c), at(h, behind, c))
            send(at(o, x, c), sibling)
            consume(at(o, x, c))
        arrive(at(hh, behind, c))
        send(at(hh, behind, c), at(h, ahead, c))
        send(at(hh, behind, c), sibling)
        consume(at(hh, behind, c))
        arrive(at(hh, ahead, c))
        send(at(hh, ahead, c), sibling)
        consume(at(hh, ahead, c))
        arrive(at(hh, across, c))
        send(at(hh, across, c), sibling)
        consume(at(hh, across, c))
        for xx in (x, ahead, behind, across):
            arrive(at(hh, xx, s))
            consume(at(hh, xx, s))

    through = acc[:, 0:RW].astype(BF16)
    a_out[...] = dot_nn(hidden_t[...], through).astype(BF16).reshape(DP, 16, RW)
    a_in[me] = a_out[me]
    exchange("dp", DP, me, a_out, a_in, r_send, r_recv, True)

    wait_bytes(b_in.at[pl.ds(0, DP - 1)], b_recv)
    b_all[mm] = jnp.sum(b_in[...], axis=0)
    exchange("mp", MP, mm, b_all, b_all, bg_send, bg_recv, False)

    grad_hidden = acc[:, RW:] + dot_nt(through[:, :RANK], a1[...])
    gg[...] = (grad_hidden * c_gate[...]).astype(BF16)
    gu[...] = (grad_hidden * c_up[...]).astype(BF16)
    stores = [
        pltpu.make_async_copy(gg, gg_hbm, store_sem.at[0]),
        pltpu.make_async_copy(gu, gu_hbm, store_sem.at[1]),
    ]
    for copy in stores:
        copy.start()

    wait_bytes(b_all.at[pl.ds(0, MP - 1)], bg_recv)
    for k in range(MP):
        gb_ref[:, k * FEAT : (k + 1) * FEAT] = b_all[k][:, :FEAT]

    wait_bytes(slots_out.at[pl.ds(0, DP - 1)], p_send)
    wait_bytes(low_out.at[pl.ds(0, MP - 1)], l_send)
    wait_bytes(low_all.at[pl.ds(0, MP - 1)], lg_send)
    wait_bytes(chunks.at[pl.ds(0, MP - 1)], g_send)
    wait_bytes(b_out.at[pl.ds(0, DP - 1)], b_send)
    wait_bytes(b_all.at[pl.ds(0, MP - 1)], bg_send)
    for copy in stores:
        copy.wait()
    wait_bytes(a_in.at[pl.ds(0, DP - 1)], r_recv)
    total = jnp.sum(a_in[...].astype(F32), axis=0)
    ga_ref[0] = total[:PIECE, :RANK]
    wait_bytes(a_out.at[pl.ds(0, DP - 1)], r_send)


def body(og, gate, up, w, a1, a2, plan):
    hbm = pl.BlockSpec(memory_space=pl.ANY)
    vmem = pl.BlockSpec(memory_space=pltpu.VMEM)
    V = pltpu.VMEM
    return tuple(pl.pallas_call(
        kernel,
        out_shape=(
            jax.ShapeDtypeStruct((TOK, HID), BF16),
            jax.ShapeDtypeStruct((TOK, HID), BF16),
            jax.ShapeDtypeStruct((1, PIECE, RANK), F32),
            jax.ShapeDtypeStruct((2, MODEL), F32),
        ),
        in_specs=[hbm] * 7,
        out_specs=(hbm, hbm, vmem, vmem),
        scratch_shapes=[
            V((TOK, FEAT), BF16),
            V((TOK, WIDE), BF16),
            V((TOK, HID), BF16),
            V((TOK, HID), BF16),
            V((HID, MODEL), BF16),
            V((HID, RANK), BF16),
            V((RANK, MODEL), BF16),
            V((1, 24), jnp.int32),
            V((DP, 8, WIDE), BF16),
            V((DP, 8, WIDE), BF16),
            V((MP, 16, RW), F32),
            V((MP, 16, RW), F32),
            V((MP, 16, RW), BF16),
            V((MP, TOK, WIDE), BF16),
            V((MP, RW + HID, WIDE), BF16),
            V((TOK, RW + HID), F32),
            V((TOK, HID), F32),
            V((TOK, HID), F32),
            V((DP * 16, TOK), BF16),
            V((DP * 8, DP * 8), BF16),
            V((TOK, HID), BF16),
            V((TOK, HID), BF16),
            V((RW, WIDE), F32),
            V((DP, 2, WIDE), F32),
            V((DP, 2, WIDE), F32),
            V((MP, 2, WIDE), F32),
            V((DP, 16, RW), BF16),
            V((DP, 16, RW), BF16),
            pltpu.SemaphoreType.DMA((7,)),
            pltpu.SemaphoreType.DMA((2,)),
            pltpu.SemaphoreType.DMA((MP,)),
            pltpu.SemaphoreType.DMA((13,)),
        ],
        compiler_params=pltpu.CompilerParams(
            collective_id=0, has_side_effects=True, vmem_limit_bytes=48 * 1024 * 1024
        ),
        name="repack_backward",
    )(og, gate, up, w, a1, a2, plan.reshape(1, 24)))


def solution(mesh):
    return jax.shard_map(
        body,
        mesh=mesh,
        in_specs=(
            P("dp", "mp"),
            P("dp", "mp"),
            P("dp", "mp"),
            P("mp", None),
            P("mp", None),
            P(),
            P("dp"),
        ),
        out_specs=(P("dp", "mp"), P("dp", "mp"), P("mp", "dp", None), P("dp", None)),
        check_vma=False,
    )
```

time: 216 us -> 74 us (0.34)
  blocking collectives: 77.6 us -> 0 us
  Pallas kernels: 0 us -> 64.9 us
  waiting for transfers between devices: 61.6 us -> 0 us
  starting transfers between devices: 53.8 us -> 0 us
  matrix products: 6.75 us -> 0 us
  local copies, waits for them, and re-layouts: 12.3 us -> 8.19 us
  other arithmetic: 2.24 us -> 0 us
    all_to_all x2 -> x0, blocking collectives: 77.6 us -> none  [the longest x1 40 us: copy_for_each(): lax.all_to_all(jnp.broadcast_to(array[None], (count, *array.shape)), axis...]
    pallas_call x0 -> x1, Pallas kernels: none -> 64.9 us  [body(): pl.pallas_call(kernel, out_shape=(jax.ShapeDtypeStruct((TOK, HID), BF16),...]
    all_to_all x4 -> x0, waiting for transfers between devices: 61.6 us -> none  [the longest x2 34.2 us: copy_for_each(): lax.all_to_all(jnp.broadcast_to(array[None], (count, *array.shape)), axis...]
    all_to_all x4 -> x0, starting transfers between devices: 53.8 us -> none  [the longest x2 29.1 us: sum_at_owner(): lax.all_to_all(pieces, axis, split_axis=0, concat_axis=0, tiled=True)]
    unnamed x9 -> x14, local copies, waits for them, and re-layouts: 0.05 us -> 7.59 us
    dot_general x8 -> x0, matrix products: 6.75 us -> none  [the longest x1 3.96 us: body(): lax.dot_general(feature_rows, down_weight, (((1,), (1,)), ((), ())), pref...]
    reshape x4 -> x0, local copies, waits for them, and re-layouts: 5.99 us -> none  [the longest x2 4.18 us: joined_along(): return jnp.moveaxis(pieces, 0, dim).reshape(lengths)]
    broadcast_in_dim x6 -> x0, local copies, waits for them, and re-layouts: 3.01 us -> none  [the longest x5 2.41 us: copy_for_each(): jnp.broadcast_to(array[None], (count, *array.shape))]
  transfers between devices with their start and end apart: 4 -> 0, of which waited for: 4 -> 0; matrix products, arithmetic and copies ran while one was open for 1% -> 0% of each run, Pallas kernels for 0% -> 0%
where the time goes in v1:
time: 74 us; the launch traced here: 73.7 us
  Pallas kernels  64.9 us (88%)
  local copies, waits for them, and re-layouts  8.19 us (11%)
    pallas_call x1, Pallas kernels, body(): pl.pallas_call(kernel, out_shape=(jax.ShapeDtypeStruct((TOK, HID), BF16),...  64.9 us
    unnamed x14, local copies, waits for them, and re-layouts  7.59 us

profile of v1, /device:TPU:1, one launch (start us, length us, event | category | flops | bytes accessed | tf_op | source)
XLA Modules:
  0.0 73.7 jit_solution(5120260526444775993)
XLA Ops:
  0.6 1.1 %copy.11.a1_hbm = bf16[624,96]{1,0:T(8,128)(2,1)S(1)} copy(bf16[624,96]{0,1:T(8,128)(2,1)} %param.11) | data formatting | bytes 239616 | tf_op args[4]
  1.7 0.0 copy-start
  1.7 1.1 %copy-done = bf16[96,3584]{1,0:T(8,128)(2,1)S(1)} copy-done((bf16[96,3584]{1,0:T(8,128)(2,1)S(1)}, bf16[96,3584]{1,0:T(8,128)(2,1)}, u32[]{:S(2)}) %copy-start) | copy-done | bytes 688152
  2.8 0.0 copy-start.1
  2.8 0.9 %copy-done.1 = bf16[192,624]{1,0:T(8,128)(2,1)S(1)} copy-done((bf16[192,624]{1,0:T(8,128)(2,1)S(1)}, bf16[192,624]{1,0:T(8,128)(2,1)}, u32[]{:S(2)}) %copy-start.1) | copy-done | bytes 239640
  3.7 0.0 copy-start.2
  3.7 0.9 %copy-done.2 = bf16[192,624]{1,0:T(8,128)(2,1)S(1)} copy-done((bf16[192,624]{1,0:T(8,128)(2,1)S(1)}, bf16[192,624]{1,0:T(8,128)(2,1)}, u32[]{:S(2)}) %copy-start.2) | copy-done | bytes 239640
  4.7 0.0 copy-start.3
  4.7 0.9 %copy-done.3 = bf16[192,224]{1,0:T(8,128)(2,1)S(1)} copy-done((bf16[192,224]{1,0:T(8,128)(2,1)S(1)}, bf16[192,224]{1,0:T(8,128)(2,1)}, u32[]{:S(2)}) %copy-start.3) | copy-done | bytes 86040
  5.6 0.0 copy-start.4
  5.6 0.7 copy-done.4
  6.2 64.9 %repack_backward.1 = (bf16[192,624]{1,0:T(8,128)(2,1)S(1)}, bf16[192,624]{1,0:T(8,128)(2,1)S(1)}, f32[1,13,96]{2,1,0:T(8,128)S(1)}, f32[2,3584]{1,0:T(2,128)S(1)}) custom-call(bf16[192,224]{1,0:T(8,128)(2,1)S(1)} %copy-done.3, bf16[192,624]{1,0:T(8,128)(2,1)S(1)} %copy-done.1, bf16[192,624]{1,0:T(8,128)(2,1)S(1)} %copy-done.2, bf16[624,3584]{1,0:T(8,128)(2,1)} %w_hbm.1, ...), custom_call_target="tpu_custom_call" | custom-call | tf_op jit(solution)/shard_map/repack_backward/pallas_call | solution.py:254
  71.1 0.6 copy.12
  71.7 0.7 copy.16
  72.4 0.7 copy.17
  73.1 0.6 copy.18
Async XLA Ops:
  1.7 1.1 %copy-start = (bf16[96,3584]{1,0:T(8,128)(2,1)S(1)}, bf16[96,3584]{1,0:T(8,128)(2,1)}, u32[]{:S(2)}) copy-start(bf16[96,3584]{1,0:T(8,128)(2,1)} %a2_hbm.1) | copy-start | bytes 2064388
  2.8 0.9 %copy-start.1 = (bf16[192,624]{1,0:T(8,128)(2,1)S(1)}, bf16[192,624]{1,0:T(8,128)(2,1)}, u32[]{:S(2)}) copy-start(bf16[192,624]{1,0:T(8,128)(2,1)} %gate_hbm.1) | copy-start | bytes 718852
  3.7 0.9 %copy-start.2 = (bf16[192,624]{1,0:T(8,128)(2,1)S(1)}, bf16[192,624]{1,0:T(8,128)(2,1)}, u32[]{:S(2)}) copy-start(bf16[192,624]{1,0:T(8,128)(2,1)} %up_hbm.1) | copy-start | bytes 718852
  4.7 0.9 %copy-start.3 = (bf16[192,224]{1,0:T(8,128)(2,1)S(1)}, bf16[192,224]{1,0:T(8,128)(2,1)}, u32[]{:S(2)}) copy-start(bf16[192,224]{1,0:T(8,128)(2,1)} %og_hbm.1) | copy-start | bytes 258052
  5.6 0.7 copy-start.4

commit v2 on v1

--- a/solution.py
+++ b/solution.py
@@ -11,6 +11,7 @@
 TOK, FEAT, WIDE = 192, 224, 256
 HID, RANK, RW = 624, 96, 128
 PIECE = 13
+NY, NZ = 4, 12
 MODEL = 3584
 
 
@@ -40,30 +41,16 @@
 
 def kernel(
     og_hbm, gate_hbm, up_hbm, w_hbm, a1_hbm, a2_hbm, plan_hbm,
-    gg_hbm, gu_hbm, ga_ref, gb_ref,
+    gg, gu, ga_ref, gb_ref,
     og, og_ext, gate, up, w, a1, a2, plan,
     slots_out, slots_in, low_out, low_in, low_all,
-    chunks, weights, acc, c_gate, c_up, hidden_t, earlier, gg, gu,
+    chunks, a2_cut, w_cut, thru, acc, c_gate, c_up, hidden_t, earlier,
     b_part, b_out, b_in, b_all, a_out, a_in,
-    load_sem, store_sem, g_recv, sems,
+    load_sem, g_recv, sems,
 ):
     me, mm = lax.axis_index("dp"), lax.axis_index("mp")
     (p_send, p_recv, l_send, l_recv, lg_send, lg_recv, g_send, b_send, b_recv,
      bg_send, bg_recv, r_send, r_recv) = [sems.at[k] for k in range(13)]
-
-    barrier = pltpu.get_barrier_semaphore()
-
-    @pl.loop(1, DP)
-    def _(i):
-        pl.semaphore_signal(
-            barrier, inc=1, device_id={"dp": lax.rem(me + i, DP)}, device_id_type=MESH
-        )
-
-    @pl.loop(1, MP)
-    def _(i):
-        pl.semaphore_signal(
-            barrier, inc=1, device_id={"mp": lax.rem(mm + i, MP)}, device_id_type=MESH
-        )
 
     loads = [
         pltpu.make_async_copy(src, dst, load_sem.at[k])
@@ -75,18 +62,48 @@
     for copy in loads:
         copy.start()
 
-    def exchange(axis, count, mine, src, dst, send_sem, recv_sem, by_peer):
-        @pl.loop(1, count)
+    barrier = pltpu.get_barrier_semaphore()
+
+    @pl.loop(1, DP)
+    def _(i):
+        pl.semaphore_signal(
+            barrier, inc=1, device_id={"dp": lax.rem(me + i, DP)}, device_id_type=MESH
+        )
+
+    @pl.loop(1, MP)
+    def _(i):
+        pl.semaphore_signal(
+            barrier, inc=1, device_id={"mp": lax.rem(mm + i, MP)}, device_id_type=MESH
+        )
+
+    def give(axis, mine, peer, src, dst, send_sem, recv_sem, by_peer):
+        pltpu.make_async_remote_copy(
+            src_ref=src.at[peer] if by_peer else src.at[mine],
+            dst_ref=dst.at[mine],
+            send_sem=send_sem,
+            recv_sem=recv_sem,
+            device_id={axis: peer},
+            device_id_type=MESH,
+        ).start()
+
+    def over_mp(src, dst, send_sem, recv_sem, by_peer):
+        @pl.loop(1, MP)
         def _(i):
-            peer = lax.rem(mine + i, count)
-            pltpu.make_async_remote_copy(
-                src_ref=src.at[peer] if by_peer else src.at[mine],
-                dst_ref=dst.at[mine],
-                send_sem=send_sem,
-                recv_sem=recv_sem,
-                device_id={axis: peer},
-                device_id_type=MESH,
-            ).start()
+            give("mp", mm, lax.rem(mm + i, MP), src, dst, send_sem, recv_sem, by_peer)
+
+    z = lax.rem(me, NZ)
+    base = [lax.rem(me // NZ + e, NY) * NZ for e in range(NY)]
+
+    def over_dp(src, dst, send_sem, recv_sem):
+        @pl.loop(0, NZ - 1)
+        def _(j):
+            step = ((j + 1) >> 1) * (2 * (j & 1) - 1)
+            there = lax.rem(z + step + (NZ + NZ // 2), NZ)
+            for e in range(NY):
+                give("dp", me, base[NY - 1 - e] + there, src, dst, send_sem, recv_sem, True)
+
+        for e in range(1, NY):
+            give("dp", me, base[NY - e] + z, src, dst, send_sem, recv_sem, True)
 
     loads[0].wait()
     expand = onehot(iota((24, TOK), 0) == (iota((24, TOK), 1) >> 3))
@@ -102,7 +119,7 @@
     slots_in[me] = slots_out[me]
 
     pl.semaphore_wait(barrier, DP - 1 + MP - 1)
-    exchange("dp", DP, me, slots_out, slots_in, p_send, p_recv, True)
+    over_dp(slots_out, slots_in, p_send, p_recv)
 
     loads[2].wait()
     loads[3].wait()
@@ -115,9 +132,9 @@
     hidden = (silu * u).astype(BF16)
     loads[4].wait()
     low_out[...] = jnp.zeros((MP, 16, RW), F32)
-    low_out[0 : TOK // 16, :, :RANK] = dot_nn(hidden, a1[...]).reshape(TOK // 16, 16, RANK)
+    low_out[0 : TOK // 16, :, :RANK] = dot_nt(hidden, a1[...]).reshape(TOK // 16, 16, RANK)
     low_in[mm] = low_out[mm]
-    exchange("mp", MP, mm, low_out, low_in, l_send, l_recv, True)
+    over_mp(low_out, low_in, l_send, l_recv, True)
 
     row = iota((DP * 16, HID), 0)
     spread = onehot(((row >> 4) * PIECE + (row & 15) == iota((DP * 16, HID), 1)) & ((row & 15) < PIECE))
@@ -129,14 +146,15 @@
     loads[6].wait()
     for k in range(MP):
         cols = slice(k * FEAT, (k + 1) * FEAT)
-        weights[k, RANK:RW, :] = jnp.zeros((RW - RANK, WIDE), BF16)
-        weights[k, :, FEAT:] = jnp.zeros((RW + HID, WIDE - FEAT), BF16)
-        weights[k, 0:RANK, :FEAT] = a2[:, cols]
-        weights[k, RW:, :FEAT] = w[:, cols]
+        a2_cut[k, RANK:, :] = jnp.zeros((RW - RANK, WIDE), BF16)
+        a2_cut[k, 0:RANK, FEAT:] = jnp.zeros((RANK, WIDE - FEAT), BF16)
+        a2_cut[k, 0:RANK, :FEAT] = a2[:, cols]
+        w_cut[k, :, FEAT:] = jnp.zeros((HID, WIDE - FEAT), BF16)
+        w_cut[k, :, :FEAT] = w[:, cols]
 
     wait_bytes(low_in.at[pl.ds(0, MP - 1)], l_recv)
     low_all[mm] = jnp.sum(low_in[...], axis=0).astype(BF16)
-    exchange("mp", MP, mm, low_all, low_all, lg_send, lg_recv, False)
+    over_mp(low_all, low_all, lg_send, lg_recv, False)
 
     wait_bytes(slots_in.at[pl.ds(0, DP - 1)], p_recv)
     arrived = slots_in[...].reshape(DP * 8, WIDE)
@@ -172,22 +190,23 @@
         wait_bytes(chunks.at[slot], g_recv.at[slot])
 
     def consume(slot):
-        acc[...] += dot_nt(chunks[slot], weights[slot])
+        thru[...] += dot_nt(chunks[slot], a2_cut[slot])
 
     sibling = at(h, x, s)
     send(mm, at(o, x, c))
     send(mm, at(h, ahead, c))
     send(mm, at(h, behind, c))
     send(mm, sibling)
-    acc[...] = dot_nt(chunks[mm], weights[mm])
-
-    wait_bytes(low_all.at[pl.ds(0, MP - 1)], lg_recv)
-    low = low_all[...].reshape(MP * 16, RW)[:TOK, :]
-    b_part[...] = dot_tn(low, packed)
-    for k in range(DP):
-        b_out[k] = b_part[2 * k : 2 * k + 2, :]
-    b_in[me] = b_out[me]
-    exchange("dp", DP, me, b_out, b_in, b_send, b_recv, True)
+    thru[...] = dot_nt(packed, a2_cut[mm])
+
+    def second_factor():
+        wait_bytes(low_all.at[pl.ds(0, MP - 1)], lg_recv)
+        low = low_all[...].reshape(MP * 16, RW)[:TOK, :]
+        b_part[...] = dot_tn(low, packed)
+        for k in range(DP):
+            b_out[k] = b_part[2 * k : 2 * k + 2, :]
+        b_in[me] = b_out[me]
+        over_dp(b_out, b_in, b_send, b_recv)
 
     for hh in (h, o):
         if hh is o:
@@ -203,6 +222,8 @@
         arrive(at(hh, ahead, c))
         send(at(hh, ahead, c), sibling)
         consume(at(hh, ahead, c))
+        if hh is h:
+            second_factor()
         arrive(at(hh, across, c))
         send(at(hh, across, c), sibling)
         consume(at(hh, across, c))
@@ -210,24 +231,24 @@
             arrive(at(hh, xx, s))
             consume(at(hh, xx, s))
 
-    through = acc[:, 0:RW].astype(BF16)
+    through = thru[...].astype(BF16)
     a_out[...] = dot_nn(hidden_t[...], through).astype(BF16).reshape(DP, 16, RW)
     a_in[me] = a_out[me]
-    exchange("dp", DP, me, a_out, a_in, r_send, r_recv, True)
+    over_dp(a_out, a_in, r_send, r_recv)
 
     wait_bytes(b_in.at[pl.ds(0, DP - 1)], b_recv)
     b_all[mm] = jnp.sum(b_in[...], axis=0)
-    exchange("mp", MP, mm, b_all, b_all, bg_send, bg_recv, False)
-
-    grad_hidden = acc[:, RW:] + dot_nt(through[:, :RANK], a1[...])
+    over_mp(b_all, b_all, bg_send, bg_recv, False)
+
+    acc[...] = dot_nn(through[:, :RANK], a1[...])
+
+    @pl.loop(0, MP)
+    def _(k):
+        acc[...] += dot_nt(chunks[k], w_cut[k])
+
+    grad_hidden = acc[...]
     gg[...] = (grad_hidden * c_gate[...]).astype(BF16)
     gu[...] = (grad_hidden * c_up[...]).astype(BF16)
-    stores = [
-        pltpu.make_async_copy(gg, gg_hbm, store_sem.at[0]),
-        pltpu.make_async_copy(gu, gu_hbm, store_sem.at[1]),
-    ]
-    for copy in stores:
-        copy.start()
 
     wait_bytes(b_all.at[pl.ds(0, MP - 1)], bg_recv)
     for k in range(MP):
@@ -239,35 +260,46 @@
     wait_bytes(chunks.at[pl.ds(0, MP - 1)], g_send)
     wait_bytes(b_out.at[pl.ds(0, DP - 1)], b_send)
     wait_bytes(b_all.at[pl.ds(0, MP - 1)], bg_send)
-    for copy in stores:
-        copy.wait()
     wait_bytes(a_in.at[pl.ds(0, DP - 1)], r_recv)
     total = jnp.sum(a_in[...].astype(F32), axis=0)
-    ga_ref[0] = total[:PIECE, :RANK]
+    ga_ref[...] = total[:PIECE, :RANK].reshape(PIECE, 1, RANK)
     wait_bytes(a_out.at[pl.ds(0, DP - 1)], r_send)
 
 
+def deliver(*refs):
+    sources, targets, sem = refs[:4], refs[4:8], refs[8]
+    copies = [
+        pltpu.make_async_copy(source, target, sem.at[k])
+        for k, (source, target) in enumerate(zip(sources, targets))
+    ]
+    for copy in copies:
+        copy.start()
+    for copy in copies:
+        copy.wait()
+
+
 def body(og, gate, up, w, a1, a2, plan):
-    hbm = pl.BlockSpec(memory_space=pl.ANY)
+    hbm = pl.BlockSpec(memory_space=pltpu.HBM)
     vmem = pl.BlockSpec(memory_space=pltpu.VMEM)
     V = pltpu.VMEM
-    return tuple(pl.pallas_call(
+    results = (
+        jax.ShapeDtypeStruct((TOK, HID), BF16),
+        jax.ShapeDtypeStruct((TOK, HID), BF16),
+        jax.ShapeDtypeStruct((PIECE, 1, RANK), F32),
+        jax.ShapeDtypeStruct((2, MODEL), F32),
+    )
+    found = pl.pallas_call(
         kernel,
-        out_shape=(
-            jax.ShapeDtypeStruct((TOK, HID), BF16),
-            jax.ShapeDtypeStruct((TOK, HID), BF16),
-            jax.ShapeDtypeStruct((1, PIECE, RANK), F32),
-            jax.ShapeDtypeStruct((2, MODEL), F32),
-        ),
+        out_shape=results,
         in_specs=[hbm] * 7,
-        out_specs=(hbm, hbm, vmem, vmem),
+        out_specs=(vmem,) * 4,
         scratch_shapes=[
             V((TOK, FEAT), BF16),
             V((TOK, WIDE), BF16),
             V((TOK, HID), BF16),
             V((TOK, HID), BF16),
             V((HID, MODEL), BF16),
-            V((HID, RANK), BF16),
+            V((RANK, HID), BF16),
             V((RANK, MODEL), BF16),
             V((1, 24), jnp.int32),
             V((DP, 8, WIDE), BF16),
@@ -276,14 +308,14 @@
             V((MP, 16, RW), F32),
             V((MP, 16, RW), BF16),
             V((MP, TOK, WIDE), BF16),
-            V((MP, RW + HID, WIDE), BF16),
-            V((TOK, RW + HID), F32),
+            V((MP, RW, WIDE), BF16),
+            V((MP, HID, WIDE), BF16),
+            V((TOK, RW), F32),
+            V((TOK, HID), F32),
             V((TOK, HID), F32),
             V((TOK, HID), F32),
             V((DP * 16, TOK), BF16),
             V((DP * 8, DP * 8), BF16),
-            V((TOK, HID), BF16),
-            V((TOK, HID), BF16),
             V((RW, WIDE), F32),
             V((DP, 2, WIDE), F32),
             V((DP, 2, WIDE), F32),
@@ -291,7 +323,6 @@
             V((DP, 16, RW), BF16),
             V((DP, 16, RW), BF16),
             pltpu.SemaphoreType.DMA((7,)),
-            pltpu.SemaphoreType.DMA((2,)),
             pltpu.SemaphoreType.DMA((MP,)),
             pltpu.SemaphoreType.DMA((13,)),
         ],
@@ -299,7 +330,20 @@
             collective_id=0, has_side_effects=True, vmem_limit_bytes=48 * 1024 * 1024
         ),
         name="repack_backward",
-    )(og, gate, up, w, a1, a2, plan.reshape(1, 24)))
+    )(*[
+        pltpu.with_memory_space_constraint(v, pltpu.HBM)
+        for v in (og, gate, up, w, a1.T, a2, plan.reshape(1, 24))
+    ])
+    gg, gu, ga, gb = pl.pallas_call(
+        deliver,
+        out_shape=results,
+        in_specs=[vmem] * 4,
+        out_specs=(hbm,) * 4,
+        scratch_shapes=[pltpu.SemaphoreType.DMA((4,))],
+        compiler_params=pltpu.CompilerParams(vmem_limit_bytes=1024 * 1024),
+        name="deliver",
+    )(*found)
+    return gg, gu, ga.reshape(1, PIECE, RANK), gb
 
 
 def solution(mesh):

time: 74 us -> 62.8 us (0.85)
  local copies, waits for them, and re-layouts: 8.19 us -> 0 us
  Pallas kernels: 64.9 us -> 62.1 us
    unnamed x14 -> x0, local copies, waits for them, and re-layouts: 7.59 us -> none
    pallas_call x1 -> x2, Pallas kernels: 64.9 us -> 62.1 us  [the longest x1 61.3 us: body(): pl.pallas_call(kernel, out_shape=results, in_specs=[hbm] * 7, out_specs=(...]
where the time goes in v2:
time: 62.8 us; the launch traced here: 62.7 us
  Pallas kernels  62.1 us (99%)
  between operations  0.64 us (1%)
    pallas_call x1, Pallas kernels, body(): pl.pallas_call(kernel, out_shape=results, in_specs=[hbm] * 7, out_specs=(...  61.3 us

profile of v2, /device:TPU:1, one launch (start us, length us, event | category | flops | bytes accessed | tf_op | source)
XLA Modules:
  0.0 62.7 jit_solution(7598349510698238089)
XLA Ops:
  0.6 61.3 %repack_backward.1 = (bf16[192,624]{1,0:T(8,128)(2,1)S(1)}, bf16[192,624]{1,0:T(8,128)(2,1)S(1)}, f32[13,1,96]{2,1,0:T(1,128)S(1)}, f32[2,3584]{1,0:T(2,128)S(1)}) custom-call(bf16[192,224]{1,0:T(8,128)(2,1)} %og_hbm.1, bf16[192,624]{1,0:T(8,128)(2,1)} %gate_hbm.1, bf16[192,624]{1,0:T(8,128)(2,1)} %up_hbm.1, bf16[624,3584]{1,0:T(8,128)(2,1)} %w_hbm.1, ...), custom_call_target="tpu_custom_call" | custom-call | tf_op jit(solution)/shard_map/repack_backward/pallas_call | solution.py:291
  61.9 0.8 %deliver.1 = (bf16[192,624]{1,0:T(8,128)(2,1)}, bf16[192,624]{1,0:T(8,128)(2,1)}, f32[13,1,96]{2,1,0:T(1,128)}, f32[2,3584]{1,0:T(2,128)}) custom-call(bf16[192,624]{1,0:T(8,128)(2,1)S(1)} %get-tuple-element.12.refs_0_, bf16[192,624]{1,0:T(8,128)(2,1)S(1)} %get-tuple-element.13.refs_1_, f32[13,1,96]{2,1,0:T(1,128)S(1)} %get-tuple-element.14.refs_2_, ...), custom_call_target="tpu_custom_call" | custom-call | tf_op jit(solution)/shard_map/deliver/pallas_call | solution.py:337

commit v3 on v2

--- a/solution.py
+++ b/solution.py
@@ -62,19 +62,30 @@
     for copy in loads:
         copy.start()
 
+    z = lax.rem(me, NZ)
+    base = [lax.rem(me // NZ + e, NY) * NZ for e in range(NY)]
+
+    def each_dp(act):
+        @pl.loop(0, NZ - 1)
+        def _(j):
+            step = ((j + 1) >> 1) * (2 * (j & 1) - 1)
+            there = lax.rem(z + step + (NZ + NZ // 2), NZ)
+            for e in range(NY):
+                act(base[NY - 1 - e] + there)
+
+        for e in range(1, NY):
+            act(base[NY - e] + z)
+
+    def each_mp(act):
+        for k in range(MP - 1):
+            off = MP // 2 + (k + 1) // 2 * (1 - 2 * (k % 2))
+            act(lax.rem(mm + off, MP))
+
     barrier = pltpu.get_barrier_semaphore()
-
-    @pl.loop(1, DP)
-    def _(i):
-        pl.semaphore_signal(
-            barrier, inc=1, device_id={"dp": lax.rem(me + i, DP)}, device_id_type=MESH
-        )
-
-    @pl.loop(1, MP)
-    def _(i):
-        pl.semaphore_signal(
-            barrier, inc=1, device_id={"mp": lax.rem(mm + i, MP)}, device_id_type=MESH
-        )
+    each_dp(lambda peer: pl.semaphore_signal(
+        barrier, inc=1, device_id={"dp": peer}, device_id_type=MESH))
+    each_mp(lambda peer: pl.semaphore_signal(
+        barrier, inc=1, device_id={"mp": peer}, device_id_type=MESH))
 
     def give(axis, mine, peer, src, dst, send_sem, recv_sem, by_peer):
         pltpu.make_async_remote_copy(
@@ -87,23 +98,10 @@
         ).start()
 
     def over_mp(src, dst, send_sem, recv_sem, by_peer):
-        @pl.loop(1, MP)
-        def _(i):
-            give("mp", mm, lax.rem(mm + i, MP), src, dst, send_sem, recv_sem, by_peer)
-
-    z = lax.rem(me, NZ)
-    base = [lax.rem(me // NZ + e, NY) * NZ for e in range(NY)]
+        each_mp(lambda peer: give("mp", mm, peer, src, dst, send_sem, recv_sem, by_peer))
 
     def over_dp(src, dst, send_sem, recv_sem):
-        @pl.loop(0, NZ - 1)
-        def _(j):
-            step = ((j + 1) >> 1) * (2 * (j & 1) - 1)
-            there = lax.rem(z + step + (NZ + NZ // 2), NZ)
-            for e in range(NY):
-                give("dp", me, base[NY - 1 - e] + there, src, dst, send_sem, recv_sem, True)
-
-        for e in range(1, NY):
-            give("dp", me, base[NY - e] + z, src, dst, send_sem, recv_sem, True)
+        each_dp(lambda peer: give("dp", me, peer, src, dst, send_sem, recv_sem, True))
 
     loads[0].wait()
     expand = onehot(iota((24, TOK), 0) == (iota((24, TOK), 1) >> 3))
@@ -165,7 +163,7 @@
     same_row = (iota((TOK, DP * 8), 0) & 7) == (iota((TOK, DP * 8), 1) & 7)
     keeping = onehot((present[0:1, :] > 0.5) & (rank[0:1, :] == place) & same_row)
     packed = dot_nn(keeping, arrived).astype(BF16)
-    chunks[mm] = packed
+    chunks[mm] = packed.reshape(2, TOK // 2, WIDE)
 
     h, x, c = mm // 8, lax.rem(mm // 2, 4), lax.rem(mm, 2)
     o, s = 1 - h, 1 - c
@@ -176,27 +174,34 @@
     def at(hh, xx, cc):
         return hh * 8 + xx * 2 + cc
 
-    def send(slot, dest):
-        pltpu.make_async_remote_copy(
-            src_ref=chunks.at[slot],
-            dst_ref=chunks.at[slot],
-            send_sem=g_send,
-            recv_sem=g_recv.at[slot],
-            device_id={"mp": dest},
-            device_id_type=MESH,
-        ).start()
-
-    def arrive(slot):
-        wait_bytes(chunks.at[slot], g_recv.at[slot])
+    def send(slot, half, *dests):
+        for dest in dests:
+            pltpu.make_async_remote_copy(
+                src_ref=chunks.at[slot, half],
+                dst_ref=chunks.at[slot, half],
+                send_sem=g_send,
+                recv_sem=g_recv.at[slot, half],
+                device_id={"mp": dest},
+                device_id_type=MESH,
+            ).start()
+
+    def arrive(slot, half):
+        wait_bytes(chunks.at[slot, half], g_recv.at[slot, half])
+
+    def whole(slot):
+        return chunks[slot].reshape(TOK, WIDE)
 
     def consume(slot):
-        thru[...] += dot_nt(chunks[slot], a2_cut[slot])
+        thru[...] += dot_nt(whole(slot), a2_cut[slot])
 
     sibling = at(h, x, s)
-    send(mm, at(o, x, c))
-    send(mm, at(h, ahead, c))
-    send(mm, at(h, behind, c))
-    send(mm, sibling)
+    fore, back = at(h, ahead, c), at(h, behind, c)
+    for half in (0, 1):
+        send(mm, half, at(o, x, c))
+    for half in (0, 1):
+        send(mm, half, fore, back)
+    for half in (0, 1):
+        send(mm, half, sibling)
     thru[...] = dot_nt(packed, a2_cut[mm])
 
     def second_factor():
@@ -208,28 +213,38 @@
         b_in[me] = b_out[me]
         over_dp(b_out, b_in, b_send, b_recv)
 
-    for hh in (h, o):
-        if hh is o:
-            arrive(at(o, x, c))
-            send(at(o, x, c), at(h, ahead, c))
-            send(at(o, x, c), at(h, behind, c))
-            send(at(o, x, c), sibling)
-            consume(at(o, x, c))
-        arrive(at(hh, behind, c))
-        send(at(hh, behind, c), at(h, ahead, c))
-        send(at(hh, behind, c), sibling)
-        consume(at(hh, behind, c))
-        arrive(at(hh, ahead, c))
-        send(at(hh, ahead, c), sibling)
-        consume(at(hh, ahead, c))
-        if hh is h:
-            second_factor()
-        arrive(at(hh, across, c))
-        send(at(hh, across, c), sibling)
-        consume(at(hh, across, c))
+    def neighbours(hh):
+        for half in (0, 1):
+            arrive(at(hh, behind, c), half)
+            send(at(hh, behind, c), half, fore, sibling)
+        for half in (0, 1):
+            arrive(at(hh, ahead, c), half)
+            send(at(hh, ahead, c), half, sibling)
+
+    def last(hh, half):
+        arrive(at(hh, across, c), half)
+        send(at(hh, across, c), half, sibling)
+
+    def add(hh):
+        for xx in (behind, ahead, across):
+            consume(at(hh, xx, c))
         for xx in (x, ahead, behind, across):
-            arrive(at(hh, xx, s))
+            for half in (0, 1):
+                arrive(at(hh, xx, s), half)
             consume(at(hh, xx, s))
+
+    neighbours(h)
+    for half in (0, 1):
+        arrive(at(o, x, c), half)
+        send(at(o, x, c), half, fore, back, sibling)
+        last(h, half)
+    second_factor()
+    consume(at(o, x, c))
+    add(h)
+    neighbours(o)
+    for half in (0, 1):
+        last(o, half)
+    add(o)
 
     through = thru[...].astype(BF16)
     a_out[...] = dot_nn(hidden_t[...], through).astype(BF16).reshape(DP, 16, RW)
@@ -244,7 +259,7 @@
 
     @pl.loop(0, MP)
     def _(k):
-        acc[...] += dot_nt(chunks[k], w_cut[k])
+        acc[...] += dot_nt(whole(k), w_cut[k])
 
     grad_hidden = acc[...]
     gg[...] = (grad_hidden * c_gate[...]).astype(BF16)
@@ -307,7 +322,7 @@
             V((MP, 16, RW), F32),
             V((MP, 16, RW), F32),
             V((MP, 16, RW), BF16),
-            V((MP, TOK, WIDE), BF16),
+            V((MP, 2, TOK // 2, WIDE), BF16),
             V((MP, RW, WIDE), BF16),
             V((MP, HID, WIDE), BF16),
             V((TOK, RW), F32),
@@ -323,7 +338,7 @@
             V((DP, 16, RW), BF16),
             V((DP, 16, RW), BF16),
             pltpu.SemaphoreType.DMA((7,)),
-            pltpu.SemaphoreType.DMA((MP,)),
+            pltpu.SemaphoreType.DMA((MP, 2)),
             pltpu.SemaphoreType.DMA((13,)),
         ],
         compiler_params=pltpu.CompilerParams(

time: 62.8 us -> 60.8 us (0.968)
  Pallas kernels: 62.1 us -> 60.1 us
    pallas_call x1, Pallas kernels: 61.3 us -> 59.3 us  [body(): pl.pallas_call(kernel, out_shape=results, in_specs=[hbm] * 7, out_specs=(...]
where the time goes in v3:
time: 60.8 us; the launch traced here: 60.7 us
  Pallas kernels  60.1 us (99%)
  between operations  0.64 us (1%)
    pallas_call x1, Pallas kernels, body(): pl.pallas_call(kernel, out_shape=results, in_specs=[hbm] * 7, out_specs=(...  59.3 us

profile of v3, /device:TPU:1, one launch (start us, length us, event | category | flops | bytes accessed | tf_op | source)
XLA Modules:
  0.0 60.7 jit_solution(11781219501668643795)
XLA Ops:
  0.6 59.3 %repack_backward.1 = (bf16[192,624]{1,0:T(8,128)(2,1)S(1)}, bf16[192,624]{1,0:T(8,128)(2,1)S(1)}, f32[13,1,96]{2,1,0:T(1,128)S(1)}, f32[2,3584]{1,0:T(2,128)S(1)}) custom-call(bf16[192,224]{1,0:T(8,128)(2,1)} %og_hbm.1, bf16[192,624]{1,0:T(8,128)(2,1)} %gate_hbm.1, bf16[192,624]{1,0:T(8,128)(2,1)} %up_hbm.1, bf16[624,3584]{1,0:T(8,128)(2,1)} %w_hbm.1, ...), custom_call_target="tpu_custom_call" | custom-call | tf_op jit(solution)/shard_map/repack_backward/pallas_call | solution.py:306
  59.9 0.8 %deliver.1 = (bf16[192,624]{1,0:T(8,128)(2,1)}, bf16[192,624]{1,0:T(8,128)(2,1)}, f32[13,1,96]{2,1,0:T(1,128)}, f32[2,3584]{1,0:T(2,128)}) custom-call(bf16[192,624]{1,0:T(8,128)(2,1)S(1)} %get-tuple-element.12.refs_0_, bf16[192,624]{1,0:T(8,128)(2,1)S(1)} %get-tuple-element.13.refs_1_, f32[13,1,96]{2,1,0:T(1,128)S(1)} %get-tuple-element.14.refs_2_, ...), custom_call_target="tpu_custom_call" | custom-call | tf_op jit(solution)/shard_map/deliver/pallas_call | solution.py:352

commit v4 on v3

--- a/solution.py
+++ b/solution.py
@@ -59,7 +59,7 @@
              (a1_hbm, a1), (a2_hbm, a2), (w_hbm, w)]
         )
     ]
-    for copy in loads:
+    for copy in loads[:2]:
         copy.start()
 
     z = lax.rem(me, NZ)
@@ -86,6 +86,8 @@
         barrier, inc=1, device_id={"dp": peer}, device_id_type=MESH))
     each_mp(lambda peer: pl.semaphore_signal(
         barrier, inc=1, device_id={"mp": peer}, device_id_type=MESH))
+    for copy in loads[2:]:
+        copy.start()
 
     def give(axis, mine, peer, src, dst, send_sem, recv_sem, by_peer):
         pltpu.make_async_remote_copy(
@@ -116,9 +118,6 @@
     slots_out[...] = dot_nn(sending, og_ext[...]).astype(BF16).reshape(DP, 8, WIDE)
     slots_in[me] = slots_out[me]
 
-    pl.semaphore_wait(barrier, DP - 1 + MP - 1)
-    over_dp(slots_out, slots_in, p_send, p_recv)
-
     loads[2].wait()
     loads[3].wait()
     g = gate[...].astype(F32)
@@ -129,9 +128,13 @@
     c_gate[...] = u * sig * (1.0 + g * (1.0 - sig))
     hidden = (silu * u).astype(BF16)
     loads[4].wait()
-    low_out[...] = jnp.zeros((MP, 16, RW), F32)
-    low_out[0 : TOK // 16, :, :RANK] = dot_nt(hidden, a1[...]).reshape(TOK // 16, 16, RANK)
+    low_out[...] = jnp.zeros((MP, 16, RW), BF16)
+    low_part = dot_nt(hidden, a1[...]).astype(BF16)
+    low_out[0 : TOK // 16, :, :RANK] = low_part.reshape(TOK // 16, 16, RANK)
     low_in[mm] = low_out[mm]
+
+    pl.semaphore_wait(barrier, DP - 1 + MP - 1)
+    over_dp(slots_out, slots_in, p_send, p_recv)
     over_mp(low_out, low_in, l_send, l_recv, True)
 
     row = iota((DP * 16, HID), 0)
@@ -151,7 +154,7 @@
         w_cut[k, :, :FEAT] = w[:, cols]
 
     wait_bytes(low_in.at[pl.ds(0, MP - 1)], l_recv)
-    low_all[mm] = jnp.sum(low_in[...], axis=0).astype(BF16)
+    low_all[mm] = jnp.sum(low_in[...].astype(F32), axis=0).astype(BF16)
     over_mp(low_all, low_all, lg_send, lg_recv, False)
 
     wait_bytes(slots_in.at[pl.ds(0, DP - 1)], p_recv)
@@ -239,9 +242,9 @@
         send(at(o, x, c), half, fore, back, sibling)
         last(h, half)
     second_factor()
+    neighbours(o)
     consume(at(o, x, c))
     add(h)
-    neighbours(o)
     for half in (0, 1):
         last(o, half)
     add(o)
@@ -319,8 +322,8 @@
             V((1, 24), jnp.int32),
             V((DP, 8, WIDE), BF16),
             V((DP, 8, WIDE), BF16),
-            V((MP, 16, RW), F32),
-            V((MP, 16, RW), F32),
+            V((MP, 16, RW), BF16),
+            V((MP, 16, RW), BF16),
             V((MP, 16, RW), BF16),
             V((MP, 2, TOK // 2, WIDE), BF16),
             V((MP, RW, WIDE), BF16),

time: 60.8 us -> 58.8 us (0.967)
  Pallas kernels: 60.1 us -> 58 us
    pallas_call x1, Pallas kernels: 59.3 us -> 57.2 us  [body(): pl.pallas_call(kernel, out_shape=results, in_specs=[hbm] * 7, out_specs=(...]
where the time goes in v4:
time: 58.8 us; the launch traced here: 58.6 us
  Pallas kernels  58 us (99%)
  between operations  0.64 us (1%)
    pallas_call x1, Pallas kernels, body(): pl.pallas_call(kernel, out_shape=results, in_specs=[hbm] * 7, out_specs=(...  57.2 us

profile of v4, /device:TPU:1, one launch (start us, length us, event | category | flops | bytes accessed | tf_op | source)
XLA Modules:
  0.0 58.6 jit_solution(825224599110560200)
XLA Ops:
  0.6 57.2 %repack_backward.1 = (bf16[192,624]{1,0:T(8,128)(2,1)S(1)}, bf16[192,624]{1,0:T(8,128)(2,1)S(1)}, f32[13,1,96]{2,1,0:T(1,128)S(1)}, f32[2,3584]{1,0:T(2,128)S(1)}) custom-call(bf16[192,224]{1,0:T(8,128)(2,1)} %og_hbm.1, bf16[192,624]{1,0:T(8,128)(2,1)} %gate_hbm.1, bf16[192,624]{1,0:T(8,128)(2,1)} %up_hbm.1, bf16[624,3584]{1,0:T(8,128)(2,1)} %w_hbm.1, ...), custom_call_target="tpu_custom_call" | custom-call | tf_op jit(solution)/shard_map/repack_backward/pallas_call | solution.py:309
  57.8 0.8 %deliver.1 = (bf16[192,624]{1,0:T(8,128)(2,1)}, bf16[192,624]{1,0:T(8,128)(2,1)}, f32[13,1,96]{2,1,0:T(1,128)}, f32[2,3584]{1,0:T(2,128)}) custom-call(bf16[192,624]{1,0:T(8,128)(2,1)S(1)} %get-tuple-element.12.refs_0_, bf16[192,624]{1,0:T(8,128)(2,1)S(1)} %get-tuple-element.13.refs_1_, f32[13,1,96]{2,1,0:T(1,128)S(1)} %get-tuple-element.14.refs_2_, ...), custom_call_target="tpu_custom_call" | custom-call | tf_op jit(solution)/shard_map/deliver/pallas_call | solution.py:355

commit v5 on v4

--- a/solution.py
+++ b/solution.py
@@ -12,6 +12,7 @@
 HID, RANK, RW = 624, 96, 128
 PIECE = 13
 NY, NZ = 4, 12
+PARTS = 3
 MODEL = 3584
 
 
@@ -166,7 +167,7 @@
     same_row = (iota((TOK, DP * 8), 0) & 7) == (iota((TOK, DP * 8), 1) & 7)
     keeping = onehot((present[0:1, :] > 0.5) & (rank[0:1, :] == place) & same_row)
     packed = dot_nn(keeping, arrived).astype(BF16)
-    chunks[mm] = packed.reshape(2, TOK // 2, WIDE)
+    chunks[mm] = packed.reshape(PARTS, TOK // PARTS, WIDE)
 
     h, x, c = mm // 8, lax.rem(mm // 2, 4), lax.rem(mm, 2)
     o, s = 1 - h, 1 - c
@@ -177,19 +178,19 @@
     def at(hh, xx, cc):
         return hh * 8 + xx * 2 + cc
 
-    def send(slot, half, *dests):
+    def send(slot, part, *dests):
         for dest in dests:
             pltpu.make_async_remote_copy(
-                src_ref=chunks.at[slot, half],
-                dst_ref=chunks.at[slot, half],
+                src_ref=chunks.at[slot, part],
+                dst_ref=chunks.at[slot, part],
                 send_sem=g_send,
-                recv_sem=g_recv.at[slot, half],
+                recv_sem=g_recv.at[slot, part],
                 device_id={"mp": dest},
                 device_id_type=MESH,
             ).start()
 
-    def arrive(slot, half):
-        wait_bytes(chunks.at[slot, half], g_recv.at[slot, half])
+    def arrive(slot, part):
+        wait_bytes(chunks.at[slot, part], g_recv.at[slot, part])
 
     def whole(slot):
         return chunks[slot].reshape(TOK, WIDE)
@@ -199,12 +200,12 @@
 
     sibling = at(h, x, s)
     fore, back = at(h, ahead, c), at(h, behind, c)
-    for half in (0, 1):
-        send(mm, half, at(o, x, c))
-    for half in (0, 1):
-        send(mm, half, fore, back)
-    for half in (0, 1):
-        send(mm, half, sibling)
+    for part in range(PARTS):
+        send(mm, part, at(o, x, c))
+    for part in range(PARTS):
+        send(mm, part, fore, back)
+    for part in range(PARTS):
+        send(mm, part, sibling)
     thru[...] = dot_nt(packed, a2_cut[mm])
 
     def second_factor():
@@ -217,36 +218,38 @@
         over_dp(b_out, b_in, b_send, b_recv)
 
     def neighbours(hh):
-        for half in (0, 1):
-            arrive(at(hh, behind, c), half)
-            send(at(hh, behind, c), half, fore, sibling)
-        for half in (0, 1):
-            arrive(at(hh, ahead, c), half)
-            send(at(hh, ahead, c), half, sibling)
-
-    def last(hh, half):
-        arrive(at(hh, across, c), half)
-        send(at(hh, across, c), half, sibling)
+        for part in range(PARTS):
+            arrive(at(hh, behind, c), part)
+            on = (fore, sibling) if hh is h else (fore, at(h, ahead, s), sibling)
+            send(at(hh, behind, c), part, *on)
+        for part in range(PARTS):
+            arrive(at(hh, ahead, c), part)
+            send(at(hh, ahead, c), part, sibling)
+
+    def last(hh, part):
+        arrive(at(hh, across, c), part)
+        if hh is h:
+            send(at(hh, across, c), part, sibling)
 
     def add(hh):
         for xx in (behind, ahead, across):
             consume(at(hh, xx, c))
         for xx in (x, ahead, behind, across):
-            for half in (0, 1):
-                arrive(at(hh, xx, s), half)
+            for part in range(PARTS):
+                arrive(at(hh, xx, s), part)
             consume(at(hh, xx, s))
 
     neighbours(h)
-    for half in (0, 1):
-        arrive(at(o, x, c), half)
-        send(at(o, x, c), half, fore, back, sibling)
-        last(h, half)
+    for part in range(PARTS):
+        arrive(at(o, x, c), part)
+        send(at(o, x, c), part, fore, back, sibling)
+        last(h, part)
     second_factor()
     neighbours(o)
     consume(at(o, x, c))
     add(h)
-    for half in (0, 1):
-        last(o, half)
+    for part in range(PARTS):
+        last(o, part)
     add(o)
 
     through = thru[...].astype(BF16)
@@ -325,7 +328,7 @@
             V((MP, 16, RW), BF16),
             V((MP, 16, RW), BF16),
             V((MP, 16, RW), BF16),
-            V((MP, 2, TOK // 2, WIDE), BF16),
+            V((MP, PARTS, TOK // PARTS, WIDE), BF16),
             V((MP, RW, WIDE), BF16),
             V((MP, HID, WIDE), BF16),
             V((TOK, RW), F32),
@@ -341,7 +344,7 @@
             V((DP, 16, RW), BF16),
             V((DP, 16, RW), BF16),
             pltpu.SemaphoreType.DMA((7,)),
-            pltpu.SemaphoreType.DMA((MP, 2)),
+            pltpu.SemaphoreType.DMA((MP, PARTS)),
             pltpu.SemaphoreType.DMA((13,)),
         ],
         compiler_params=pltpu.CompilerParams(

time: 58.8 us -> 58.3 us (level)
  no operation moved by 1% of the time
where the time goes in v5:
time: 58.3 us; the launch traced here: 58.1 us
  Pallas kernels  57.5 us (99%)
  between operations  0.64 us (1%)
    pallas_call x1, Pallas kernels, body(): pl.pallas_call(kernel, out_shape=results, in_specs=[hbm] * 7, out_specs=(...  56.6 us

profile of v5, /device:TPU:1, one launch (start us, length us, event | category | flops | bytes accessed | tf_op | source)
XLA Modules:
  0.0 58.1 jit_solution(1833676354802100371)
XLA Ops:
  0.6 56.6 %repack_backward.1 = (bf16[192,624]{1,0:T(8,128)(2,1)S(1)}, bf16[192,624]{1,0:T(8,128)(2,1)S(1)}, f32[13,1,96]{2,1,0:T(1,128)S(1)}, f32[2,3584]{1,0:T(2,128)S(1)}) custom-call(bf16[192,224]{1,0:T(8,128)(2,1)} %og_hbm.1, bf16[192,624]{1,0:T(8,128)(2,1)} %gate_hbm.1, bf16[192,624]{1,0:T(8,128)(2,1)} %up_hbm.1, bf16[624,3584]{1,0:T(8,128)(2,1)} %w_hbm.1, ...), custom_call_target="tpu_custom_call" | custom-call | tf_op jit(solution)/shard_map/repack_backward/pallas_call | solution.py:312
  57.3 0.8 %deliver.1 = (bf16[192,624]{1,0:T(8,128)(2,1)}, bf16[192,624]{1,0:T(8,128)(2,1)}, f32[13,1,96]{2,1,0:T(1,128)}, f32[2,3584]{1,0:T(2,128)}) custom-call(bf16[192,624]{1,0:T(8,128)(2,1)S(1)} %get-tuple-element.12.refs_0_, bf16[192,624]{1,0:T(8,128)(2,1)S(1)} %get-tuple-element.13.refs_1_, f32[13,1,96]{2,1,0:T(1,128)S(1)} %get-tuple-element.14.refs_2_, ...), custom_call_target="tpu_custom_call" | custom-call | tf_op jit(solution)/shard_map/deliver/pallas_call | solution.py:358
